TPU v7x, 32 devices: a whole 2x2x4 slice. The times are simulated.
32 devices in a mesh: src: 8 (over z, y), reg: 4 (over x, core).
Axes of the slice: x: 2, y: 2, z: 4, core: 2. Of those that a mesh axis runs over, the one named last changes fastest.
Arguments:
- tiles: bfloat16 [16384, 128, 128], P(('src', 'reg')), may hold values from -0.1875 to 0.1875
- rays: float32 [2048, 128], P(('src', 'reg')), may hold values from -6 to 6
- tile_rows: int32 [16384], P(('src', 'reg')), may hold values from 0 to 63, as said below
- tile_slots: int32 [16384], P(('src', 'reg')), may hold values from 0 to 63, as said below
- tile_count: int32 [32], P(('src', 'reg')), may hold values from 64 to 512, as said below
- wanted: int32 [32, 32, 2], P(('src', 'reg')), may hold values from 0 to 255
Outputs:
- solution: float32 [8192, 128], P(('src', 'reg'))
- right_vector: float32 [8192, 128], P(('src', 'reg'))
Inputs may be any that keep to these rules, and one draw needn't show every extreme that they name: `tile_rows`: non-decreasing along each device's 512 tiles. `tile_slots`: the first 64 tiles of each device name every slot once. `tile_count`: some device has all 512 tiles live.
All inputs are finite; a program needn't handle non-finite values.
Results may differ from a plain program's by a relative error of at most 0.024.
Values may be sent and summed in bfloat16 or wider, within the bound.
A program may use at most 128 MiB of HBM per device.

v0:
```python
import functools

import jax
import jax.numpy as jnp
from jax import lax
from jax.experimental import pallas as pl
from jax.experimental.pallas import tpu as pltpu
from jax.sharding import PartitionSpec as P

BLK_DEV = 256
ITERS = 3
damping = 0.5

GROUP = 16
HALF = GROUP // 2
F32 = jnp.float32
BF16 = jnp.bfloat16
MESH = pl.DeviceIdType.MESH


def one_hot_dot(hot, x, parts=2):
    total = None
    for part in range(parts):
        piece = x.astype(BF16)
        prod = jnp.dot(hot, piece, preferred_element_type=F32)
        total = prod if total is None else total + prod
        if part < parts - 1:
            x = x - piece.astype(F32)
    return total


def kernel(
    n, regs, stride, cap, chunks,
    tiles_hbm, rays_ref, rows_row, rows_col, slots_row, slots_col, req_row, req_col,
    sol_ref, right_ref,
    tiles_ref, left_ref, mid_ref, slot_hot, slot_hot_t, ray_hot, ray_hot_t, same_ref,
    send_ref, recv_ref, tile_sem, send_sem, recv_sem,
):
    src = lax.axis_index("src")
    reg = lax.axis_index("reg")
    me = src * regs + reg
    count = tiles_ref.shape[0]
    width = tiles_ref.shape[2]
    per_chunk = count // chunks
    groups = count // GROUP
    rows = n * stride
    row_blocks = rays_ref.shape[0]

    def tile_copy(c):
        part = pl.ds(c * per_chunk, per_chunk)
        return pltpu.make_async_copy(tiles_hbm.at[part], tiles_ref.at[part], tile_sem.at[c])

    for c in range(chunks):
        tile_copy(c).start()

    barrier = pltpu.get_barrier_semaphore()

    @pl.loop(1, n)
    def _(k):
        d = lax.rem(me + k, n)
        pl.semaphore_signal(
            barrier, inc=1, device_id=(d // regs, lax.rem(d, regs)), device_id_type=MESH
        )

    def hot(a, b):
        return jnp.where(a == b, 1.0, 0.0).astype(BF16)

    iota = functools.partial(lax.broadcasted_iota, jnp.int32)
    slot_hot[...] = hot(iota((rows, count), 0), slots_row[...])
    slot_hot_t[...] = hot(iota((count, rows), 1), slots_col[...])
    ray_hot[...] = hot(iota((row_blocks, count), 0), rows_row[...])
    ray_hot_t[...] = hot(iota((count, row_blocks), 1), rows_col[...])
    same = (req_col[...] == req_row[...]) & (req_col[...] >= 0)
    same_ref[...] = jnp.where(same, 1.0, 0.0).astype(BF16)
    lower = jnp.where(same & (iota((rows, rows), 1) < iota((rows, rows), 0)), 1.0, 0.0)
    upper = jnp.where(same & (iota((rows, rows), 0) < iota((rows, rows), 1)), 1.0, 0.0)
    first_col = jnp.where(jnp.sum(lower, axis=1, keepdims=True) == 0.0, 1.0, 0.0)
    first_row = jnp.where(jnp.sum(upper, axis=0, keepdims=True) == 0.0, 1.0, 0.0)
    place = lax.rem(iota((rows, width), 0), stride)
    is_sum = place == cap

    spot = lax.rem(iota((GROUP, width), 0), HALF)
    masks = [jnp.where(spot == b, 1.0, 0.0).astype(BF16) for b in range(HALF)]

    def spread(g):
        base = pl.multiple_of(g * GROUP, GROUP)
        left = left_ref[pl.ds(base, GROUP), :]
        return base, jnp.concatenate([left * m for m in masks], axis=1)

    def keep(base, out):
        mid_ref[pl.ds(base, HALF), :] = out[:HALF, :width]
        mid_ref[pl.ds(pl.multiple_of(base + HALF, HALF), HALF), :] = out[HALF:, width:]

    def adjoint_group(g):
        base, left = spread(g)
        a = tiles_ref[pl.ds(base, HALF)].reshape(HALF * width, width)
        b = tiles_ref[pl.ds(base + HALF, HALF)].reshape(HALF * width, width)
        right = jnp.concatenate([a, b], axis=1)
        keep(base, jnp.dot(left, right, preferred_element_type=F32))

    def forward_group(g):
        base, left = spread(g)
        halves = [
            jnp.concatenate([tiles_ref[base + h * HALF + b] for b in range(HALF)], axis=1)
            for h in range(2)
        ]
        right = jnp.concatenate(halves, axis=0)
        keep(
            base,
            lax.dot_general(
                left, right, (((1,), (1,)), ((), ())), preferred_element_type=F32
            ),
        )

    def exchange(phase, value, during=None):
        send_ref[phase] = value.reshape(n, stride, width)

        @pl.loop(1, n)
        def _(k):
            d = lax.rem(me + k, n)
            pltpu.make_async_remote_copy(
                src_ref=send_ref.at[phase, d],
                dst_ref=recv_ref.at[phase, me],
                send_sem=send_sem.at[phase],
                recv_sem=recv_sem.at[phase],
                device_id=(d // regs, lax.rem(d, regs)),
                device_id_type=MESH,
            ).start()

        recv_ref[phase, me] = send_ref[phase, me]
        others = pl.ds(0, n - 1)
        pltpu.make_async_copy(
            recv_ref.at[phase, others], recv_ref.at[phase, others], recv_sem.at[phase]
        ).wait()
        got = recv_ref[phase].reshape(rows, width)
        return got, jnp.sum(jnp.where(is_sum, got, 0.0), keepdims=True)

    uraw = rays_ref[...]
    u = None
    v = w = update = jnp.zeros((rows, width), F32)
    alpha = phibar = rhobar = None
    fetched = None
    for step in range(ITERS + 1):
        if step > 0:
            left_ref[...] = jnp.dot(
                slot_hot_t[...], fetched.astype(BF16), preferred_element_type=F32
            ).astype(BF16)

            @pl.loop(0, groups, unroll=2)
            def _(g):
                forward_group(g)

            uraw = one_hot_dot(ray_hot[...], mid_ref[...]) / alpha - alpha * u
        left_ref[...] = jnp.dot(
            ray_hot_t[...], uraw.astype(BF16), preferred_element_type=F32
        ).astype(BF16)
        if step == 0:
            per = groups // chunks

            @pl.loop(0, chunks)
            def _(c):
                tile_copy(c).wait()
                for i in range(per):
                    adjoint_group(c * per + i)
        else:

            @pl.loop(0, groups, unroll=2)
            def _(g):
                adjoint_group(g)

        sums = one_hot_dot(slot_hot[...], mid_ref[...])
        squares = jnp.sum(uraw * uraw, axis=0, keepdims=True)
        if step == 0:
            pl.semaphore_wait(barrier, n - 1)
        got, uu = exchange(2 * step, jnp.where(is_sum, squares, sums))
        beta = jnp.sqrt(uu)
        u = uraw / beta
        vraw = one_hot_dot(same_ref[...], got) / beta
        if step > 0:
            vraw = vraw - beta * v
        squares = jnp.sum(vraw * vraw * first_col, axis=0, keepdims=True)
        fetched, vv = exchange(2 * step + 1, jnp.where(is_sum, squares, vraw))
        alpha = jnp.sqrt(vv)
        v = jnp.where(place < cap, vraw, 0.0) / alpha
        if step == 0:
            w = v
            phibar = beta
            rhobar = alpha
        else:
            rhobar1 = jnp.sqrt(rhobar * rhobar + damping * damping)
            phibar = rhobar / rhobar1 * phibar
            rho = jnp.sqrt(rhobar1 * rhobar1 + beta * beta)
            cosine = rhobar1 / rho
            sine = beta / rho
            theta = sine * alpha
            rhobar = -cosine * alpha
            phi = cosine * phibar
            phibar = sine * phibar
            update = update + phi / rho * w
            w = v - theta / rho * w
    blocks = sol_ref.shape[0]
    out_hot = jnp.where(
        iota((blocks, rows), 0) == req_row[...], first_row, 0.0
    ).astype(BF16)
    scale = float(blocks * width * n) ** 0.5
    sol_ref[...] = one_hot_dot(out_hot, update, 3)
    right_ref[...] = one_hot_dot(out_hot, v * scale, 3)
    for phase in range(2 * (ITERS + 1)):
        others = pl.ds(0, n - 1)
        pltpu.make_async_copy(
            send_ref.at[phase, others], send_ref.at[phase, others], send_sem.at[phase]
        ).wait()


def per_device(n, regs, tiles, rays, tile_rows, tile_slots, tile_count, wanted):
    count, width = tiles.shape[0], tiles.shape[2]
    cap = wanted.shape[2]
    stride = 4
    while stride < cap + 1:
        stride *= 2
    rows = n * stride
    chunks = 16
    phases = 2 * (ITERS + 1)
    row_blocks = rays.shape[0]
    live = jnp.arange(count, dtype=jnp.int32) < tile_count[0]
    ray_ids = jnp.where(live, tile_rows, -1)
    slot_ids = jnp.where(live, tile_slots // cap * stride + tile_slots % cap, -1)
    requests = jnp.pad(wanted[0], ((0, 0), (0, stride - cap)), constant_values=-1).reshape(-1)
    vmem = pl.BlockSpec(memory_space=pltpu.VMEM)
    out = jax.ShapeDtypeStruct((BLK_DEV, width), F32)
    return pl.pallas_call(
        functools.partial(kernel, n, regs, stride, cap, chunks),
        out_shape=(out, out),
        in_specs=[pl.BlockSpec(memory_space=pl.ANY)] + [vmem] * 7,
        out_specs=(vmem, vmem),
        scratch_shapes=[
            pltpu.VMEM(tiles.shape, BF16),
            pltpu.VMEM((count, width), BF16),
            pltpu.VMEM((count, width), F32),
            pltpu.VMEM((rows, count), BF16),
            pltpu.VMEM((count, rows), BF16),
            pltpu.VMEM((row_blocks, count), BF16),
            pltpu.VMEM((count, row_blocks), BF16),
            pltpu.VMEM((rows, rows), BF16),
            pltpu.VMEM((phases, n, stride, width), F32),
            pltpu.VMEM((phases, n, stride, width), F32),
            pltpu.SemaphoreType.DMA((chunks,)),
            pltpu.SemaphoreType.DMA((phases,)),
            pltpu.SemaphoreType.DMA((phases,)),
        ],
        compiler_params=pltpu.CompilerParams(
            collective_id=0, has_side_effects=True, vmem_limit_bytes=56 * 1024 * 1024
        ),
    )(
        tiles,
        rays,
        ray_ids[None, :],
        ray_ids[:, None],
        slot_ids[None, :],
        slot_ids[:, None],
        requests[None, :],
        requests[:, None],
    )


def solution(mesh):
    both = ("src", "reg")
    in_specs = (
        P(both, None, None),
        P(both, None),
        P(both),
        P(both),
        P(both),
        P(both, None, None),
    )
    out_specs = (P(both, None), P(both, None))
    n = mesh.shape["src"] * mesh.shape["reg"]
    return jax.shard_map(
        functools.partial(per_device, n, mesh.shape["reg"]),
        mesh=mesh,
        in_specs=in_specs,
        out_specs=out_specs,
        check_vma=False,
    )
```

profile of v0, /device:TPU:0, one launch (start us, length us, event | category | flops | bytes accessed | tf_op | source)
XLA Modules:
  0.0 91.5 jit_solution(9463924721101725956)
XLA Ops:
  1.3 0.7 fusion.2
  2.0 0.0 copy-start
  2.0 0.0 copy-start.1
  2.0 0.8 copy.16
  2.8 0.7 broadcast_in_dim_reshape.6.req_row
  3.5 0.7 broadcast_in_dim_reshape.8.req_col
  4.2 0.8 copy.13.rows_col
  5.0 0.8 copy.14.slots_col
  5.9 0.0 copy-done
  5.9 0.0 copy-done.1
  5.9 82.5 %shard_map.77 = (f32[256,128]{1,0:T(8,128)}, f32[256,128]{1,0:T(8,128)}) custom-call(bf16[512,128,128]{2,1,0:T(8,128)(2,1)} %tiles_hbm.1, f32[64,128]{1,0:T(8,128)} %rays_ref.1, s32[1,512]{1,0:T(1,128)} %bitcast.10, s32[512,1]{1,0:T(8,128)} %copy.13.rows_col, s32[1,512]{1,0:T(1,128)} %bitcast.8, s32[512,1]{1,0:T(8,128)} %copy.14.slots_col, ...), custom_call_target="tpu_custom_call" | custom-call | tf_op jit(solution)/shard_map/pallas_call | solution.py:231
  88.3 1.6 %copy.20 = f32[256,128]{1,0:T(8,128)} copy(f32[256,128]{1,0:T(8,128)} %get-tuple-element.6) | data formatting | bytes 262144
  89.9 1.6 %copy.21 = f32[256,128]{1,0:T(8,128)} copy(f32[256,128]{1,0:T(8,128)} %get-tuple-element.7) | data formatting | bytes 262144
  (1 shorter events, 0.0 us)
Async XLA Ops:
  2.0 3.9 %copy-start = (s32[512]{0:T(512)}, s32[512]{0:T(512)S(1)}, u32[]{:S(2)}) copy-start(s32[512]{0:T(512)S(1)} %get-tuple-element.2) | copy-start | bytes 6148
  2.0 3.9 %copy-start.1 = (s32[512]{0:T(512)}, s32[512]{0:T(512)S(1)}, u32[]{:S(2)}) copy-start(s32[512]{0:T(512)S(1)} %get-tuple-element.3) | copy-start | bytes 6148
where the time goes:
time: 91.7 us; the launch traced here: 91.5 us
  Pallas kernels  82.5 us (90%)
  local copies, waits for them, and re-layouts  6.99 us (8%)
  between operations  1.31 us (1%)
    pallas_call x1, Pallas kernels, per_device(): pl.pallas_call(functools.partial(kernel, n, regs, stride, cap, chunks), o...  82.5 us
    unnamed x7, local copies, waits for them, and re-layouts  3.91 us

commit v1 on v0

--- a/solution.py
+++ b/solution.py
@@ -13,6 +13,7 @@
 
 GROUP = 16
 HALF = GROUP // 2
+TURN = 4
 F32 = jnp.float32
 BF16 = jnp.bfloat16
 MESH = pl.DeviceIdType.MESH
@@ -31,9 +32,9 @@
 
 def kernel(
     n, regs, stride, cap, chunks,
-    tiles_hbm, rays_ref, rows_row, rows_col, slots_row, slots_col, req_row, req_col,
+    count_ref, tiles_hbm, rays_ref, rows_ref, slots_ref, wanted_ref,
     sol_ref, right_ref,
-    tiles_ref, left_ref, mid_ref, slot_hot, slot_hot_t, ray_hot, ray_hot_t, same_ref,
+    tiles_ref, turned_ref, left_ref, mid_ref, slot_hot, slot_hot_t, ray_hot, ray_hot_t, same_ref,
     send_ref, recv_ref, tile_sem, send_sem, recv_sem,
 ):
     src = lax.axis_index("src")
@@ -66,11 +67,31 @@
         return jnp.where(a == b, 1.0, 0.0).astype(BF16)
 
     iota = functools.partial(lax.broadcasted_iota, jnp.int32)
-    slot_hot[...] = hot(iota((rows, count), 0), slots_row[...])
-    slot_hot_t[...] = hot(iota((count, rows), 1), slots_col[...])
-    ray_hot[...] = hot(iota((row_blocks, count), 0), rows_row[...])
-    ray_hot_t[...] = hot(iota((count, row_blocks), 1), rows_col[...])
-    same = (req_col[...] == req_row[...]) & (req_col[...] >= 0)
+    live = iota((1, count), 1) < count_ref[0]
+    slots = slots_ref[...]
+    slots = jnp.where(live, slots // cap * stride + lax.rem(slots, cap), -1)
+    one_slot = hot(iota((rows, count), 0), slots)
+    one_ray = hot(iota((row_blocks, count), 0), jnp.where(live, rows_ref[...], -1))
+    slot_hot[...] = one_slot
+    slot_hot_t[...] = one_slot.T
+    ray_hot[...] = one_ray
+    ray_hot_t[...] = one_ray.T
+    wanted = wanted_ref[...].astype(F32)
+    row_place = lax.rem(iota((1, rows), 1), stride)
+    col_place = lax.rem(iota((rows, 1), 0), stride)
+    peers_t = jnp.where(iota((n, rows), 0) == iota((n, rows), 1) // stride, 1.0, 0.0)
+    peers = jnp.where(iota((rows, n), 1) == iota((rows, n), 0) // stride, 1.0, 0.0)
+    req_row = jnp.where(row_place < cap, 0.0, -1.0)
+    req_col = jnp.where(col_place < cap, 0.0, -1.0)
+    for k in range(cap):
+        asked = wanted[k : k + 1, :]
+        req_col += jnp.where(col_place == k, jnp.sum(peers * asked, axis=1, keepdims=True), 0.0)
+        picked = jnp.dot(
+            jnp.broadcast_to(asked, (8, n)), peers_t, preferred_element_type=F32,
+            precision=lax.Precision.HIGHEST,
+        )[:1]
+        req_row += jnp.where(row_place == k, picked, 0.0)
+    same = (req_col == req_row) & (req_col >= 0.0)
     same_ref[...] = jnp.where(same, 1.0, 0.0).astype(BF16)
     lower = jnp.where(same & (iota((rows, rows), 1) < iota((rows, rows), 0)), 1.0, 0.0)
     upper = jnp.where(same & (iota((rows, rows), 0) < iota((rows, rows), 1)), 1.0, 0.0)
@@ -91,33 +112,23 @@
         mid_ref[pl.ds(base, HALF), :] = out[:HALF, :width]
         mid_ref[pl.ds(pl.multiple_of(base + HALF, HALF), HALF), :] = out[HALF:, width:]
 
-    def adjoint_group(g):
+    def group(source, g):
         base, left = spread(g)
-        a = tiles_ref[pl.ds(base, HALF)].reshape(HALF * width, width)
-        b = tiles_ref[pl.ds(base + HALF, HALF)].reshape(HALF * width, width)
+        a = source[pl.ds(base, HALF)].reshape(HALF * width, width)
+        b = source[pl.ds(base + HALF, HALF)].reshape(HALF * width, width)
         right = jnp.concatenate([a, b], axis=1)
         keep(base, jnp.dot(left, right, preferred_element_type=F32))
 
-    def forward_group(g):
-        base, left = spread(g)
-        halves = [
-            jnp.concatenate([tiles_ref[base + h * HALF + b] for b in range(HALF)], axis=1)
-            for h in range(2)
-        ]
-        right = jnp.concatenate(halves, axis=0)
-        keep(
-            base,
-            lax.dot_general(
-                left, right, (((1,), (1,)), ((), ())), preferred_element_type=F32
-            ),
-        )
+    upper_half = me >= n // 2
+    skip = jnp.where(upper_half, me, n - 1 - me)
 
     def exchange(phase, value, during=None):
         send_ref[phase] = value.reshape(n, stride, width)
 
-        @pl.loop(1, n)
-        def _(k):
-            d = lax.rem(me + k, n)
+        @pl.loop(0, n - 1)
+        def _(j):
+            j = j + jnp.where(j >= skip, 1, 0)
+            d = jnp.where(upper_half, j, n - 1 - j)
             pltpu.make_async_remote_copy(
                 src_ref=send_ref.at[phase, d],
                 dst_ref=recv_ref.at[phase, me],
@@ -148,7 +159,7 @@
 
             @pl.loop(0, groups, unroll=2)
             def _(g):
-                forward_group(g)
+                group(turned_ref, g)
 
             uraw = one_hot_dot(ray_hot[...], mid_ref[...]) / alpha - alpha * u
         left_ref[...] = jnp.dot(
@@ -161,12 +172,16 @@
             def _(c):
                 tile_copy(c).wait()
                 for i in range(per):
-                    adjoint_group(c * per + i)
+                    group(tiles_ref, c * per + i)
+
+                @pl.loop(0, per_chunk, unroll=TURN)
+                def _(i):
+                    turned_ref[c * per_chunk + i] = tiles_ref[c * per_chunk + i].T
         else:
 
             @pl.loop(0, groups, unroll=2)
             def _(g):
-                adjoint_group(g)
+                group(tiles_ref, g)
 
         sums = one_hot_dot(slot_hot[...], mid_ref[...])
         squares = jnp.sum(uraw * uraw, axis=0, keepdims=True)
@@ -200,7 +215,7 @@
             w = v - theta / rho * w
     blocks = sol_ref.shape[0]
     out_hot = jnp.where(
-        iota((blocks, rows), 0) == req_row[...], first_row, 0.0
+        iota((blocks, rows), 0).astype(F32) == req_row, first_row, 0.0
     ).astype(BF16)
     scale = float(blocks * width * n) ** 0.5
     sol_ref[...] = one_hot_dot(out_hot, update, 3)
@@ -222,18 +237,19 @@
     chunks = 16
     phases = 2 * (ITERS + 1)
     row_blocks = rays.shape[0]
-    live = jnp.arange(count, dtype=jnp.int32) < tile_count[0]
-    ray_ids = jnp.where(live, tile_rows, -1)
-    slot_ids = jnp.where(live, tile_slots // cap * stride + tile_slots % cap, -1)
-    requests = jnp.pad(wanted[0], ((0, 0), (0, stride - cap)), constant_values=-1).reshape(-1)
     vmem = pl.BlockSpec(memory_space=pltpu.VMEM)
     out = jax.ShapeDtypeStruct((BLK_DEV, width), F32)
     return pl.pallas_call(
         functools.partial(kernel, n, regs, stride, cap, chunks),
         out_shape=(out, out),
-        in_specs=[pl.BlockSpec(memory_space=pl.ANY)] + [vmem] * 7,
+        in_specs=[
+            pl.BlockSpec(memory_space=pltpu.SMEM),
+            pl.BlockSpec(memory_space=pl.ANY),
+        ]
+        + [vmem] * 4,
         out_specs=(vmem, vmem),
         scratch_shapes=[
+            pltpu.VMEM(tiles.shape, BF16),
             pltpu.VMEM(tiles.shape, BF16),
             pltpu.VMEM((count, width), BF16),
             pltpu.VMEM((count, width), F32),
@@ -252,14 +268,12 @@
             collective_id=0, has_side_effects=True, vmem_limit_bytes=56 * 1024 * 1024
         ),
     )(
+        tile_count,
         tiles,
         rays,
-        ray_ids[None, :],
-        ray_ids[:, None],
-        slot_ids[None, :],
-        slot_ids[:, None],
-        requests[None, :],
-        requests[:, None],
+        tile_rows[None, :],
+        tile_slots[None, :],
+        wanted[0].T,
     )
 
 

time: 91.7 us -> 89.9 us (0.980)
  local copies, waits for them, and re-layouts: 6.99 us -> 3.14 us
  Pallas kernels: 82.5 us -> 85.2 us
    pallas_call x1, Pallas kernels: 82.5 us -> 85.2 us  [per_device(): pl.pallas_call(functools.partial(kernel, n, regs, stride, cap, chunks), o...]
    broadcast_in_dim x2 -> x0, local copies, waits for them, and re-layouts: 1.69 us -> none  [the longest x1 0.85 us: per_device(): ray_ids[:, None]]
    another operation x2 -> x0, local copies, waits for them, and re-layouts: 1.38 us -> none  [the longest x1 0.71 us: per_device(): requests[:, None]]
    unnamed x7 -> x2, local copies, waits for them, and re-layouts: 3.91 us -> 3.14 us
where the time goes in v1:
time: 89.9 us; the launch traced here: 89.6 us
  Pallas kernels  85.2 us (95%)
  local copies, waits for them, and re-layouts  3.14 us (3%)
  between operations  1.29 us (1%)
    pallas_call x1, Pallas kernels, per_device(): pl.pallas_call(functools.partial(kernel, n, regs, stride, cap, chunks), o...  85.2 us
    unnamed x2, local copies, waits for them, and re-layouts  3.14 us

profile of v1, /device:TPU:0, one launch (start us, length us, event | category | flops | bytes accessed | tf_op | source)
XLA Modules:
  0.0 89.6 jit_solution(12608433197308763397)
XLA Ops:
  1.3 85.2 %shard_map.77 = (f32[256,128]{1,0:T(8,128)}, f32[256,128]{1,0:T(8,128)}) custom-call(s32[1]{0:T(128)S(6)} %copy.10.count_ref, bf16[512,128,128]{2,1,0:T(8,128)(2,1)} %tiles_hbm.1, f32[64,128]{1,0:T(8,128)} %rays_ref.1, s32[1,512]{1,0:T(1,128)} %bitcast.5, s32[1,512]{1,0:T(1,128)} %bitcast.6, s32[2,32]{1,0:T(2,128)} %bitcast.7), custom_call_target="tpu_custom_call" | custom-call | tf_op jit(solution)/shard_map/pallas_call | solution.py:242
  86.5 1.6 %copy.11 = f32[256,128]{1,0:T(8,128)} copy(f32[256,128]{1,0:T(8,128)} %get-tuple-element.4) | data formatting | bytes 262144
  88.1 1.6 %copy.12 = f32[256,128]{1,0:T(8,128)} copy(f32[256,128]{1,0:T(8,128)} %get-tuple-element.5) | data formatting | bytes 262144

commit v2 on v1

--- a/solution.py
+++ b/solution.py
@@ -13,7 +13,6 @@
 
 GROUP = 16
 HALF = GROUP // 2
-TURN = 4
 F32 = jnp.float32
 BF16 = jnp.bfloat16
 MESH = pl.DeviceIdType.MESH
@@ -98,7 +97,15 @@
     first_col = jnp.where(jnp.sum(lower, axis=1, keepdims=True) == 0.0, 1.0, 0.0)
     first_row = jnp.where(jnp.sum(upper, axis=0, keepdims=True) == 0.0, 1.0, 0.0)
     place = lax.rem(iota((rows, width), 0), stride)
-    is_sum = place == cap
+    is_high = place == cap
+    is_low = place == cap + 1
+    is_sum = is_high | is_low
+
+    def packed(value, squares):
+        high = squares.astype(BF16).astype(F32)
+        value = jnp.where(is_high, high, value)
+        return jnp.where(is_low, squares - high, value).astype(BF16)
+
 
     spot = lax.rem(iota((GROUP, width), 0), HALF)
     masks = [jnp.where(spot == b, 1.0, 0.0).astype(BF16) for b in range(HALF)]
@@ -122,7 +129,7 @@
     upper_half = me >= n // 2
     skip = jnp.where(upper_half, me, n - 1 - me)
 
-    def exchange(phase, value, during=None):
+    def exchange(phase, value):
         send_ref[phase] = value.reshape(n, stride, width)
 
         @pl.loop(0, n - 1)
@@ -144,7 +151,9 @@
             recv_ref.at[phase, others], recv_ref.at[phase, others], recv_sem.at[phase]
         ).wait()
         got = recv_ref[phase].reshape(rows, width)
-        return got, jnp.sum(jnp.where(is_sum, got, 0.0), keepdims=True)
+        return got, jnp.sum(
+            jnp.where(is_sum, got.astype(F32), 0.0), keepdims=True
+        )
 
     uraw = rays_ref[...]
     u = None
@@ -154,7 +163,7 @@
     for step in range(ITERS + 1):
         if step > 0:
             left_ref[...] = jnp.dot(
-                slot_hot_t[...], fetched.astype(BF16), preferred_element_type=F32
+                slot_hot_t[...], fetched, preferred_element_type=F32
             ).astype(BF16)
 
             @pl.loop(0, groups, unroll=2)
@@ -174,9 +183,9 @@
                 for i in range(per):
                     group(tiles_ref, c * per + i)
 
-                @pl.loop(0, per_chunk, unroll=TURN)
-                def _(i):
-                    turned_ref[c * per_chunk + i] = tiles_ref[c * per_chunk + i].T
+                for i in range(per_chunk):
+                    t = c * per_chunk + i
+                    turned_ref[t] = tiles_ref[t].T
         else:
 
             @pl.loop(0, groups, unroll=2)
@@ -187,14 +196,14 @@
         squares = jnp.sum(uraw * uraw, axis=0, keepdims=True)
         if step == 0:
             pl.semaphore_wait(barrier, n - 1)
-        got, uu = exchange(2 * step, jnp.where(is_sum, squares, sums))
+        got, uu = exchange(2 * step, packed(sums, squares))
         beta = jnp.sqrt(uu)
         u = uraw / beta
-        vraw = one_hot_dot(same_ref[...], got) / beta
+        vraw = jnp.dot(same_ref[...], got, preferred_element_type=F32) / beta
         if step > 0:
             vraw = vraw - beta * v
         squares = jnp.sum(vraw * vraw * first_col, axis=0, keepdims=True)
-        fetched, vv = exchange(2 * step + 1, jnp.where(is_sum, squares, vraw))
+        fetched, vv = exchange(2 * step + 1, packed(vraw, squares))
         alpha = jnp.sqrt(vv)
         v = jnp.where(place < cap, vraw, 0.0) / alpha
         if step == 0:
@@ -231,7 +240,7 @@
     count, width = tiles.shape[0], tiles.shape[2]
     cap = wanted.shape[2]
     stride = 4
-    while stride < cap + 1:
+    while stride < cap + 2:
         stride *= 2
     rows = n * stride
     chunks = 16
@@ -258,8 +267,8 @@
             pltpu.VMEM((row_blocks, count), BF16),
             pltpu.VMEM((count, row_blocks), BF16),
             pltpu.VMEM((rows, rows), BF16),
-            pltpu.VMEM((phases, n, stride, width), F32),
-            pltpu.VMEM((phases, n, stride, width), F32),
+            pltpu.VMEM((phases, n, stride, width), BF16),
+            pltpu.VMEM((phases, n, stride, width), BF16),
             pltpu.SemaphoreType.DMA((chunks,)),
             pltpu.SemaphoreType.DMA((phases,)),
             pltpu.SemaphoreType.DMA((phases,)),

time: 89.9 us -> 79.5 us (0.88)
  Pallas kernels: 85.2 us -> 74.9 us
    pallas_call x1, Pallas kernels: 85.2 us -> 74.9 us  [per_device(): pl.pallas_call(functools.partial(kernel, n, regs, stride, cap, chunks), o...]
where the time goes in v2:
time: 79.5 us; the launch traced here: 79.3 us
  Pallas kernels  74.9 us (94%)
  local copies, waits for them, and re-layouts  3.14 us (4%)
  between operations  1.29 us (2%)
    pallas_call x1, Pallas kernels, per_device(): pl.pallas_call(functools.partial(kernel, n, regs, stride, cap, chunks), o...  74.9 us
    unnamed x2, local copies, waits for them, and re-layouts  3.14 us

profile of v2, /device:TPU:0, one launch (start us, length us, event | category | flops | bytes accessed | tf_op | source)
XLA Modules:
  0.0 79.3 jit_solution(1373161553253514144)
XLA Ops:
  1.3 74.9 %shard_map.77 = (f32[256,128]{1,0:T(8,128)}, f32[256,128]{1,0:T(8,128)}) custom-call(s32[1]{0:T(128)S(6)} %copy.10.count_ref, bf16[512,128,128]{2,1,0:T(8,128)(2,1)} %tiles_hbm.1, f32[64,128]{1,0:T(8,128)} %rays_ref.1, s32[1,512]{1,0:T(1,128)} %bitcast.5, s32[1,512]{1,0:T(1,128)} %bitcast.6, s32[2,32]{1,0:T(2,128)} %bitcast.7), custom_call_target="tpu_custom_call" | custom-call | tf_op jit(solution)/shard_map/pallas_call | solution.py:251
  76.2 1.6 %copy.11 = f32[256,128]{1,0:T(8,128)} copy(f32[256,128]{1,0:T(8,128)} %get-tuple-element.4) | data formatting | bytes 262144
  77.7 1.6 %copy.12 = f32[256,128]{1,0:T(8,128)} copy(f32[256,128]{1,0:T(8,128)} %get-tuple-element.5) | data formatting | bytes 262144
